TPU v7x, 32 devices: a whole 2x2x4 slice. The times are simulated.
32 devices in a mesh: dp: 4 (over y, x), expert: 4 (over z), tensor: 2 (over core).
Axes of the slice: x: 2, y: 2, z: 4, core: 2. Of those that a mesh axis runs over, the one named last changes fastest.
Arguments:
- tokens_in: bfloat16 [12608, 512], P(('dp', 'expert')), may hold values from -6 to 6
- expert_ids: int32 [12608, 2], P(('dp', 'expert')), may hold values from 0 to 7, all different within a row; in each aligned block of 788 rows (0 to 787, 788 to 1575, ...) at most 248 rows name the same one
- combine: float32 [12608, 2], P(('dp', 'expert')), may hold values from 0.2 to 1
- out_cot: float32 [12608, 512], P(('dp', 'expert')), may hold values from -6 to 6
- inward_master: float32 [512, 1536], P('dp', 'tensor'), may hold values from -0.25 to 0.25
- outward_master: float32 [512, 512], P('dp', 'tensor'), may hold values from -1 to 1
- up_master: float32 [512, 8, 2048], P('dp', 'expert', 'tensor'), may hold values from -0.25 to 0.25
- down_master: float32 [512, 8, 2048], P('dp', 'expert', 'tensor'), may hold values from -0.125 to 0.125
- norm_gains: float32 [2, 512], replicated, may hold values from 0.5 to 1.5
- norm_biases: float32 [2, 512], replicated, may hold values from -2 to 2
- inward_moment: float32 [512, 1536], P('dp', 'tensor'), may hold values from -32 to 32
- outward_moment: float32 [512, 512], P('dp', 'tensor'), may hold values from -64 to 64
- up_moment: float32 [512, 8, 2048], P('dp', 'expert', 'tensor'), may hold values from -64 to 64
- down_moment: float32 [512, 8, 2048], P('dp', 'expert', 'tensor'), may hold values from -64 to 64
- first_moment: float32 [4, 512], replicated, may hold values from -64 to 64
- second_moment: float32 [4, 512], replicated, may hold values from 2.5216 to 25.216
- step_count: int32 [1], replicated, may hold values from 1 to 20
Outputs:
- block_out: bfloat16 [12608, 512], P(('dp', 'expert'))
- input_gradient: float32 [12608, 512], P(('dp', 'expert'))
- inward_gradient: float32 [512, 1536], P('dp', 'tensor')
- outward_gradient: float32 [512, 512], P('dp', 'tensor')
- up_gradient: float32 [512, 8, 2048], P('dp', 'expert', 'tensor')
- down_gradient: float32 [512, 8, 2048], P('dp', 'expert', 'tensor')
- gain_gradient: float32 [2, 512], replicated
- bias_gradient: float32 [2, 512], replicated
- inward_moment_new: float32 [512, 1536], P('dp', 'tensor')
- outward_moment_new: float32 [512, 512], P('dp', 'tensor')
- up_moment_new: float32 [512, 8, 2048], P('dp', 'expert', 'tensor')
- down_moment_new: float32 [512, 8, 2048], P('dp', 'expert', 'tensor')
- inward_new: float32 [512, 1536], P('dp', 'tensor')
- outward_new: float32 [512, 512], P('dp', 'tensor')
- up_new: float32 [512, 8, 2048], P('dp', 'expert', 'tensor')
- down_new: float32 [512, 8, 2048], P('dp', 'expert', 'tensor')
- inward_copy: bfloat16 [512, 1536], P('dp', 'tensor')
- outward_copy: bfloat16 [512, 512], P('dp', 'tensor')
- up_copy: bfloat16 [512, 8, 2048], P('dp', 'expert', 'tensor')
- down_copy: bfloat16 [512, 8, 2048], P('dp', 'expert', 'tensor')
- gains_new: float32 [2, 512], replicated
- biases_new: float32 [2, 512], replicated
- first_new: float32 [4, 512], replicated
- second_new: float32 [4, 512], replicated
Inputs may be any that keep to these rules, and one draw needn't show every extreme that they name: `expert_ids`: the two ids of a row differ. Within the 788 rows of one device, no expert is named by more than 248 rows, a bound that some block reaches.
All inputs are finite; a program needn't handle non-finite values.
Results may differ from a plain program's by a relative error of at most 0.0095.
The roundings to bfloat16 on the way count: a program that leaves them out, or rounds other values in their place, can miss the bound.
Values may be sent and summed in bfloat16 or wider, within the bound.
A program may use at most 192 MiB of HBM per device.

v0:
```python
import functools
import math

import jax
import jax.numpy as jnp
import numpy as np
from jax import lax
from jax.experimental import pallas as pl
from jax.experimental.pallas import tpu as pltpu
from jax.sharding import PartitionSpec as P

D = 512
HD = 64
F = 2048
SEQ = 197
EXP_DEV = 2


def layer_norm(values, gain_row, bias_row):
    center = values - jnp.mean(values, axis=-1, keepdims=True)
    invert = lax.rsqrt(jnp.mean(center * center, axis=-1, keepdims=True) + 1e-06)
    scaled = center * invert
    return (scaled * gain_row + bias_row, scaled, invert)


def norm_backward(upstream, scaled, invert, gain_row):
    weighted = upstream * gain_row
    return invert * (
        weighted
        - jnp.mean(weighted, axis=-1, keepdims=True)
        - scaled * jnp.mean(weighted * scaled, axis=-1, keepdims=True)
    )


def gelu_exact(values):
    return 0.5 * values * (1.0 + lax.erf(values * 0.7071067811865476))


def gelu_slope(values):
    return 0.5 * (
        1.0 + lax.erf(values * 0.7071067811865476)
    ) + values * 0.3989422804014327 * jnp.exp(-0.5 * values * values)


def newton_schulz(matrix):
    current = matrix / (jnp.sqrt(jnp.sum(matrix * matrix)) + 1e-07)
    for sweep_index in range(5):
        gram_matrix = jnp.dot(current, current.T, precision=lax.Precision.HIGHEST)
        polynom = -4.775 * gram_matrix + 2.0315 * jnp.dot(
            gram_matrix, gram_matrix, precision=lax.Precision.HIGHEST
        )
        current = 3.4445 * current + jnp.dot(polynom, current, precision=lax.Precision.HIGHEST)
    return current


def start_body(
    tokens_in,
    expert_ids,
    combine,
    out_cot,
    inward_master,
    outward_master,
    up_master,
    down_master,
    norm_gains,
    norm_biases,
    inward_moment,
    outward_moment,
    up_moment,
    down_moment,
    first_moment,
    second_moment,
    step_count,
):
    dp_count = lax.axis_size("dp")
    expert_count = lax.axis_size("expert")
    tensor_count = lax.axis_size("tensor")
    token_rows = tokens_in.shape[0]
    expert_total = EXP_DEV * expert_count
    capacity = (token_rows * 10 // (4 * expert_total) + 7) // 8 * 8
    slot_total = expert_total * capacity
    inputs = tokens_in.astype(jnp.float32)
    w_inward, w_outward, w_up, w_down = (
        lax.all_gather(inward_master.astype(jnp.bfloat16), "dp", axis=0, tiled=True),
        lax.all_gather(outward_master.astype(jnp.bfloat16), "dp", axis=0, tiled=True),
        lax.all_gather(up_master.astype(jnp.bfloat16), "dp", axis=0, tiled=True),
        lax.all_gather(down_master.astype(jnp.bfloat16), "dp", axis=0, tiled=True),
    )
    expert_lanes = jnp.arange(expert_total, dtype=jnp.int32)
    route_hits = (expert_ids[:, :, None] == expert_lanes).astype(jnp.int32)
    per_token = jnp.sum(route_hits, axis=1)
    earlier = jnp.cumsum(per_token, axis=0) - per_token
    position = jnp.sum(route_hits * earlier[:, None, :], axis=2)
    target = expert_ids * capacity + position
    select = (target[:, :, None] == jnp.arange(slot_total, dtype=jnp.int32)).astype(jnp.bfloat16)
    normed1, scaled1, invert1 = layer_norm(inputs, norm_gains[0], norm_biases[0])
    normed1_low = normed1.astype(jnp.bfloat16)
    qkv_low = jnp.dot(normed1_low, w_inward, preferred_element_type=jnp.float32).astype(
        jnp.bfloat16
    )
    heads_here = w_inward.shape[1] // (3 * HD)
    images = token_rows // SEQ
    split_heads = qkv_low.reshape(images, SEQ, heads_here, 3, HD)
    query_part = split_heads[:, :, :, 0]
    key_part = split_heads[:, :, :, 1]
    value_part = split_heads[:, :, :, 2]
    score_scale = HD ** (-0.5)
    scores = (
        jnp.einsum("bihd,bjhd->bhij", query_part, key_part, preferred_element_type=jnp.float32)
        * score_scale
    )
    row_max = jnp.max(scores, axis=-1, keepdims=True)
    exponent = jnp.exp(scores - row_max)
    row_total = jnp.sum(exponent, axis=-1, keepdims=True)
    softmax_out = exponent / row_total
    softmax_low = softmax_out.astype(jnp.bfloat16)
    heads_out = (
        jnp.einsum("bhij,bjhd->bihd", softmax_low, value_part, preferred_element_type=jnp.float32)
        .astype(jnp.bfloat16)
        .reshape(token_rows, heads_here * HD)
    )
    attend_part = jnp.einsum("tc,dc->td", heads_out, w_outward, preferred_element_type=jnp.float32)
    attended = lax.psum(attend_part, "tensor")
    state = inputs + attended
    normed2, scaled2, invert2 = layer_norm(state, norm_gains[1], norm_biases[1])
    normed2_low = normed2.astype(jnp.bfloat16)
    slots_out = jnp.einsum(
        "tks,td->sd", select, normed2_low, preferred_element_type=jnp.float32
    ).astype(jnp.bfloat16)
    arrived = lax.all_to_all(
        slots_out.reshape(expert_count, EXP_DEV, capacity, D),
        "expert",
        split_axis=0,
        concat_axis=0,
        tiled=True,
    )
    pre_act = jnp.einsum("secd,def->secf", arrived, w_up, preferred_element_type=jnp.float32)
    hidden_low = gelu_exact(pre_act).astype(jnp.bfloat16)
    expert_part = jnp.einsum(
        "secf,def->secd", hidden_low, w_down, preferred_element_type=jnp.float32
    ).astype(jnp.bfloat16)
    returned = lax.all_to_all(expert_part, "expert", split_axis=0, concat_axis=0, tiled=True)
    routed = jnp.einsum(
        "tks,sd->tkd", select, returned.reshape(slot_total, D), preferred_element_type=jnp.float32
    )
    mixed_part = jnp.sum(routed * combine[:, :, None], axis=1)
    mixed_sum = lax.psum(mixed_part, "tensor")
    block_out = (state + mixed_sum).astype(jnp.bfloat16)
    routed_grad = (combine[:, :, None] * out_cot[:, None, :]).astype(jnp.bfloat16)
    slot_grad = jnp.einsum(
        "tks,tkd->sd", select, routed_grad, preferred_element_type=jnp.float32
    ).astype(jnp.bfloat16)
    grad_arrived = lax.all_to_all(
        slot_grad.reshape(expert_count, EXP_DEV, capacity, D),
        "expert",
        split_axis=0,
        concat_axis=0,
        tiled=True,
    )
    hidden_grad = jnp.einsum(
        "secd,def->secf", grad_arrived, w_down, preferred_element_type=jnp.float32
    )
    pre_grad = (hidden_grad * gelu_slope(pre_act)).astype(jnp.bfloat16)
    down_local = jnp.einsum(
        "secd,secf->def", grad_arrived, hidden_low, preferred_element_type=jnp.float32
    )
    up_local = jnp.einsum("secd,secf->def", arrived, pre_grad, preferred_element_type=jnp.float32)
    entry_grad = jnp.einsum(
        "secf,def->secd", pre_grad, w_up, preferred_element_type=jnp.float32
    ).astype(jnp.bfloat16)
    entry_back = lax.all_to_all(entry_grad, "expert", split_axis=0, concat_axis=0, tiled=True)
    normed2_part = jnp.einsum(
        "tks,sd->td", select, entry_back.reshape(slot_total, D), preferred_element_type=jnp.float32
    )
    normed2_grad = lax.psum(normed2_part, "tensor")
    state_grad = out_cot + norm_backward(normed2_grad, scaled2, invert2, norm_gains[1])
    state_low = state_grad.astype(jnp.bfloat16)
    outward_local = jnp.einsum(
        "td,tc->dc", state_low, heads_out, preferred_element_type=jnp.float32
    )
    heads_grad = (
        jnp.dot(state_low, w_outward, preferred_element_type=jnp.float32)
        .astype(jnp.bfloat16)
        .reshape(images, SEQ, heads_here, HD)
    )
    prob_grad = jnp.einsum(
        "bihd,bjhd->bhij", heads_grad, value_part, preferred_element_type=jnp.float32
    )
    score_grad = (
        softmax_out * (prob_grad - jnp.sum(softmax_out * prob_grad, axis=-1, keepdims=True))
    ).astype(jnp.bfloat16)
    query_grad = (
        jnp.einsum("bhij,bjhd->bihd", score_grad, key_part, preferred_element_type=jnp.float32)
        * score_scale
    )
    key_grad = (
        jnp.einsum("bhij,bihd->bjhd", score_grad, query_part, preferred_element_type=jnp.float32)
        * score_scale
    )
    value_grad = jnp.einsum(
        "bhij,bihd->bjhd", softmax_low, heads_grad, preferred_element_type=jnp.float32
    )
    qkv_grad = (
        jnp.stack([query_grad, key_grad, value_grad], axis=3)
        .reshape(token_rows, heads_here * 3 * HD)
        .astype(jnp.bfloat16)
    )
    inward_local = jnp.einsum(
        "td,tc->dc", normed1_low, qkv_grad, preferred_element_type=jnp.float32
    )
    normed1_part = jnp.einsum("tc,dc->td", qkv_grad, w_inward, preferred_element_type=jnp.float32)
    normed1_grad = lax.psum(normed1_part, "tensor")
    input_gradient = state_grad + norm_backward(normed1_grad, scaled1, invert1, norm_gains[0])
    norm_terms = jnp.stack(
        [
            jnp.sum(normed1_grad * scaled1, axis=0),
            jnp.sum(normed2_grad * scaled2, axis=0),
            jnp.sum(normed1_grad, axis=0),
            jnp.sum(normed2_grad, axis=0),
        ]
    )
    inward_total, outward_total, norm_total = lax.psum(
        (inward_local, outward_local, norm_terms), ("dp", "expert")
    )
    up_gradient, down_gradient = (
        lax.psum_scatter(up_local, "dp", scatter_dimension=0, tiled=True),
        lax.psum_scatter(down_local, "dp", scatter_dimension=0, tiled=True),
    )
    shard_rows = D // dp_count
    dp_here = lax.axis_index("dp")
    inward_gradient = lax.dynamic_slice_in_dim(inward_total, dp_here * shard_rows, shard_rows, 0)
    outward_gradient = lax.dynamic_slice_in_dim(outward_total, dp_here * shard_rows, shard_rows, 0)
    inward_next = 0.95 * inward_moment + inward_gradient
    outward_next = 0.95 * outward_moment + outward_gradient
    up_next = 0.95 * up_moment + up_gradient
    down_next = 0.95 * down_moment + down_gradient
    matrices = [up_next[:, expert_slot] for expert_slot in range(EXP_DEV)]
    matrices = matrices + [down_next[:, expert_slot] for expert_slot in range(EXP_DEV)]
    matrices = matrices + [jnp.concatenate([inward_next, outward_next], axis=1)]
    stacked = jnp.stack(matrices)
    slot_count = len(matrices)
    group_size = dp_count * tensor_count
    shard_width = stacked.shape[2]
    query_cols = inward_next.shape[1]

    def orth_expert(pieces):
        whole_matrix = pieces.transpose(0, 2, 1, 3).reshape(D, tensor_count * shard_width)
        result = newton_schulz(whole_matrix) * (0.2 * math.sqrt(F))
        return result.reshape(dp_count, shard_rows, tensor_count, shard_width).transpose(0, 2, 1, 3)

    def orth_attention(pieces):
        inward_whole = (
            pieces[..., :query_cols].transpose(0, 2, 1, 3).reshape(D, tensor_count * query_cols)
        )
        outward_whole = (
            pieces[..., query_cols:]
            .transpose(0, 2, 1, 3)
            .reshape(D, tensor_count * (shard_width - query_cols))
        )
        inward_result = newton_schulz(inward_whole) * (0.2 * math.sqrt(3 * D))
        outward_result = newton_schulz(outward_whole) * (0.2 * math.sqrt(D))
        inward_blocks = inward_result.reshape(
            dp_count, shard_rows, tensor_count, query_cols
        ).transpose(0, 2, 1, 3)
        outward_blocks = outward_result.reshape(
            dp_count, shard_rows, tensor_count, shard_width - query_cols
        ).transpose(0, 2, 1, 3)
        return jnp.concatenate([inward_blocks, outward_blocks], axis=3)

    owner_index = lax.axis_index(("dp", "tensor"))
    outgoing = stacked[np.arange(group_size) % slot_count]
    received = lax.all_to_all(outgoing, ("dp", "tensor"), split_axis=0, concat_axis=0, tiled=True)
    blocks = received.reshape(dp_count, tensor_count, shard_rows, shard_width)
    slot_here = owner_index % slot_count
    result_blocks = lax.cond(slot_here == slot_count - 1, orth_attention, orth_expert, blocks)
    arrived_steps = lax.all_to_all(
        result_blocks.reshape(group_size, shard_rows, shard_width),
        ("dp", "tensor"),
        split_axis=0,
        concat_axis=0,
        tiled=True,
    )
    picked = []
    for owned_slot in range(slot_count):
        replicas = (group_size - owned_slot + slot_count - 1) // slot_count
        source = owned_slot + slot_count * (owner_index % replicas)
        picked.append(lax.dynamic_index_in_dim(arrived_steps, source, 0, keepdims=False))
    up_step = jnp.stack(picked[0:EXP_DEV], axis=1)
    down_step = jnp.stack(picked[EXP_DEV : 2 * EXP_DEV], axis=1)
    attend_step = picked[2 * EXP_DEV]
    inward_new = inward_master - 0.1 * (attend_step[:, :query_cols] + 0.1 * inward_master)
    outward_new = outward_master - 0.1 * (attend_step[:, query_cols:] + 0.1 * outward_master)
    up_new = up_master - 0.1 * (up_step + 0.1 * up_master)
    down_new = down_master - 0.1 * (down_step + 0.1 * down_master)
    moment_first = 0.9 * first_moment + 0.1 * norm_total
    moment_second = 0.999 * second_moment + 0.001 * norm_total * norm_total
    steps_done = step_count[0].astype(jnp.float32)
    direction = (
        moment_first
        / (1.0 - jnp.power(0.9, steps_done))
        / (jnp.sqrt(moment_second / (1.0 - jnp.power(0.999, steps_done))) + 1e-08)
    )
    params_new = jnp.concatenate([norm_gains, norm_biases], axis=0) - 0.1 * direction
    return (
        block_out,
        input_gradient,
        inward_gradient,
        outward_gradient,
        up_gradient,
        down_gradient,
        norm_total[0:2],
        norm_total[2:4],
        inward_next,
        outward_next,
        up_next,
        down_next,
        inward_new,
        outward_new,
        up_new,
        down_new,
        inward_new.astype(jnp.bfloat16),
        outward_new.astype(jnp.bfloat16),
        up_new.astype(jnp.bfloat16),
        down_new.astype(jnp.bfloat16),
        params_new[0:2],
        params_new[2:4],
        moment_first,
        moment_second,
    )


PAIRS = (1, 2, 3)
FAR_FIRST = (3, 2, 1, 0)
MIDWAY = 1
LANES = 128
NOWHERE = 128 * 128 - 1
PAD = 208
NT = (((1,), (1,)), ((), ()))
TN = (((0,), (0,)), ((), ()))


def mxu(left, right, dims=(((1,), (0,)), ((), ()))):
    return lax.dot_general(left, right, dims, preferred_element_type=jnp.float32)


def spread_rows(value, padded_ref):
    padded_ref[...] = jnp.zeros_like(padded_ref)
    for image in range(value.shape[0] // SEQ):
        padded_ref[image * PAD : image * PAD + SEQ, :] = value[image * SEQ : (image + 1) * SEQ]


def gather_rows(padded, out_ref):
    for image in range(out_ref.shape[0] // SEQ):
        out_ref[image * SEQ : (image + 1) * SEQ, :] = padded[
            image * PAD : image * PAD + SEQ
        ].astype(out_ref.dtype)


def peer(me, k):
    return (me + k) % 2 + 2 * ((me // 2 + k // 2) % 2)


def remote(source, target, send, recv, device):
    copy = pltpu.make_async_remote_copy(
        src_ref=source,
        dst_ref=target,
        send_sem=send,
        recv_sem=recv,
        device_id=device,
        device_id_type=pl.DeviceIdType.MESH,
    )
    copy.start()
    return copy


class Copy:
    def __init__(self, parts, start=True):
        self.parts = parts
        if start:
            self.make().start()

    def make(self):
        source, target, send, recv, device = self.parts()
        return pltpu.make_async_remote_copy(
            src_ref=source,
            dst_ref=target,
            send_sem=send,
            recv_sem=recv,
            device_id=device,
            device_id_type=pl.DeviceIdType.MESH,
        )

    def wait_recv(self):
        self.make().wait_recv()

    def wait_send(self):
        self.make().wait_send()


def keep(source, target, sem):
    copy = pltpu.make_async_copy(source, target, sem)
    copy.start()
    return copy


def greet(dp_here, expert_here, core, over_expert=True):
    barrier = pltpu.get_barrier_semaphore()
    devices = [{"dp": peer(dp_here, k)} for k in PAIRS] + [{"tensor": 1 - core}]
    if over_expert:
        devices += [{"expert": peer(expert_here, k)} for k in PAIRS]
    for device in devices:
        pl.semaphore_signal(
            barrier, inc=1, device_id=device, device_id_type=pl.DeviceIdType.MESH
        )
    return lambda: pl.semaphore_wait(barrier, len(devices))


def block_rows(index, size):
    return pl.ds(pl.multiple_of(index * size, size), size)


def one_hot(cond):
    return jnp.where(cond, 1.0, 0.0).astype(jnp.bfloat16)


def route(ids, capacity, target_ref, target_t_ref):
    rows = ids.shape[0]
    square = (PAD, PAD)
    below = one_hot(
        lax.broadcasted_iota(jnp.int32, square, 0) > lax.broadcasted_iota(jnp.int32, square, 1)
    )
    lane = lax.broadcasted_iota(jnp.int32, (rows, 128), 1)
    hits = one_hot((lane == ids[:, 0:1]) | (lane == ids[:, 1:2]))
    earlier, passed = [], jnp.zeros((1, 128), jnp.float32)
    for image in range(rows // PAD):
        own = hits[image * PAD : (image + 1) * PAD]
        earlier.append(mxu(below, own) + passed)
        passed += jnp.sum(own.astype(jnp.float32), axis=0, keepdims=True)
    earlier = jnp.concatenate(earlier, axis=0)
    target = jnp.zeros((rows, 128), jnp.int32)
    parts = jnp.zeros((rows, 128), jnp.int32)
    for r in range(2):
        own = ids[:, r : r + 1]
        position = jnp.sum(jnp.where(lane == own, earlier, 0.0), axis=1, keepdims=True)
        value = jnp.where(own >= 0, own * capacity + position.astype(jnp.int32), NOWHERE)
        target = jnp.where(lane == r, value, target)
        parts = jnp.where(lane == 2 * r, value // 128, jnp.where(lane == 2 * r + 1, value % 128, parts))
    target_ref[...] = target
    identity = one_hot(
        lax.broadcasted_iota(jnp.int32, (8, 128), 0) == lax.broadcasted_iota(jnp.int32, (8, 128), 1)
    )
    flipped = mxu(identity, parts.astype(jnp.float32).astype(jnp.bfloat16), NT).astype(jnp.int32)
    for r in range(2):
        target_t_ref[r : r + 1, :] = flipped[2 * r : 2 * r + 1] * 128 + flipped[2 * r + 1 : 2 * r + 2]


def attend(qkv_ref, probs_ref, gift_ref):
    heads_here = qkv_ref.shape[1] // (3 * HD)
    key_lane = lax.broadcasted_iota(jnp.int32, (PAD, PAD), 1)

    def one_image(image, carry):
        rows = block_rows(image, PAD)
        out_rows = pl.ds(pl.multiple_of(D + image * PAD, 16), PAD)
        for head in range(heads_here):
            base = head * 3 * HD
            query = qkv_ref[rows, base : base + HD]
            key = qkv_ref[rows, base + HD : base + 2 * HD]
            value = qkv_ref[rows, base + 2 * HD : base + 3 * HD]
            scores = jnp.where(key_lane < SEQ, mxu(query, key, NT) * HD ** (-0.5), -1e30)
            exponent = jnp.exp(scores - jnp.max(scores, axis=-1, keepdims=True))
            probs = exponent / jnp.sum(exponent, axis=-1, keepdims=True)
            probs_ref[image * heads_here + head] = probs
            gift_ref[out_rows, head * HD : (head + 1) * HD] = mxu(
                probs.astype(jnp.bfloat16), value
            ).astype(jnp.bfloat16)
        return carry

    lax.fori_loop(0, qkv_ref.shape[0] // PAD, one_image, 0)


def woven(array):
    rows, count, width = array.shape
    tiles = array.reshape(rows, count, width // LANES, LANES)
    return tiles.transpose(0, 2, 1, 3).reshape(-1, LANES)


def unwoven(array, whole):
    rows, count, width = whole
    tiles = array.reshape(rows, width // LANES, count, LANES)
    return tiles.transpose(0, 2, 1, 3).reshape(whole)


def strand(tile, expert, rows, width):
    step = EXP_DEV * (width // LANES)
    return pl.ds(EXP_DEV * tile + expert, rows, stride=step)


def front_kernel(
    ids_ref,
    combine_ref,
    cot_ref,
    tokens_ref,
    gains_ref,
    biases_ref,
    inward_ref,
    outward_ref,
    up_ref,
    down_ref,
    up_moment_ref,
    down_moment_ref,
    state_ref,
    gift_ref,
    qkv_ref,
    probs_ref,
    weight_ref,
    target_ref,
    combine_out_ref,
    moment_shard,
    expert_w_ref,
    arrived_ref,
    grad_arrived_ref,
    padded,
    columns,
    columns_padded,
    raw,
    target_t_ref,
    attend_shard,
    expert_shard,
    gift_other_ref,
    grad_chunks,
    token_chunks,
    inner_send,
    inner_recv,
    expert_send,
    expert_recv,
    slot_send,
    slot_recv,
    share_send,
    share_recv,
    gift_sems,
    keep_sems,
    raw_sems,
):
    bf16 = jnp.bfloat16
    dp_here, expert_here, core = (lax.axis_index(a) for a in ("dp", "expert", "tensor"))
    partner = {"tensor": 1 - core}
    capacity = grad_chunks.shape[1]
    shard_rows = attend_shard.shape[0]
    qcols = qkv_ref.shape[1]
    width = attend_shard.shape[1]
    here = block_rows(dp_here, shard_rows)
    ready = greet(dp_here, expert_here, core)
    loads = [
        keep(ref, raw.at[place], raw_sems.at[place])
        for place, ref in enumerate((up_ref, down_ref, up_moment_ref, down_moment_ref))
    ]

    def unpick(place, tile, expert):
        return raw[place, strand(tile, expert, shard_rows, width), :].astype(bf16)

    attend_shard[:, :qcols] = inward_ref[...].astype(bf16)
    attend_shard[:, qcols:] = outward_ref[...].astype(bf16)
    weight_ref[here, :] = attend_shard[...]
    ready()
    inner = [
        remote(
            attend_shard,
            weight_ref.at[here, :],
            inner_send.at[k - 1],
            inner_recv.at[k - 1],
            {"dp": peer(dp_here, k)},
        )
        for k in PAIRS
    ]
    kept = []

    rest = combine_ref[...]
    for part in range(3):
        piece = rest.astype(bf16).astype(jnp.float32)
        columns[2 * part : 2 * part + 2, :] = piece
        rest = rest - piece
    columns[6:8, :] = (ids_ref[...] + 1).astype(jnp.float32)
    identity = one_hot(
        lax.broadcasted_iota(jnp.int32, (8, 128), 0) == lax.broadcasted_iota(jnp.int32, (8, 128), 1)
    )
    spread_rows(mxu(columns[...].astype(bf16), identity, TN), columns_padded)
    for r in range(2):
        combine_out_ref[:, r : r + 1] = (
            columns_padded[:, r : r + 1]
            + columns_padded[:, 2 + r : 3 + r]
            + columns_padded[:, 4 + r : 5 + r]
        )
    ids = columns_padded[...].astype(jnp.int32) - 1
    route(ids[:, 6:8], capacity, target_ref, target_t_ref)
    spread_rows(cot_ref[...], padded)
    slot = lax.broadcasted_iota(jnp.int32, (capacity, padded.shape[0]), 0)

    def first_slot(k):
        return (2 * peer(expert_here, k) + core) * capacity

    def send_chunks(fill, chunks, landing, which):
        def going(k, start=True):
            return Copy(
                lambda: (
                    chunks.at[k],
                    landing.at[0, k],
                    slot_send.at[which, k],
                    slot_recv.at[which, k],
                    {"expert": peer(expert_here, k)},
                ),
                start,
            )

        def make(k):
            chunks[k] = fill(slot + first_slot(k)).astype(bf16)

        def make_and_send(step, carry):
            make(2 - step)
            going(3 - step)
            return carry

        make(3)
        lax.fori_loop(0, 3, make_and_send, 0)
        copies, shared = {k: going(k, start=False) for k in PAIRS}, []
        kept.append(keep(chunks.at[0], landing.at[0, 0], keep_sems.at[1 + which]))
        shared.append(
            remote(
                chunks.at[0],
                landing.at[1, 0],
                share_send.at[which, 0],
                share_recv.at[which, 0],
                partner,
            )
        )
        return copies, shared

    def share_arrivals(copies, landing, which, shared):
        for k in FAR_FIRST[:3]:
            copies[k].wait_recv()
            shared.append(
                remote(
                    landing.at[0, k],
                    landing.at[1, k],
                    share_send.at[which, k],
                    share_recv.at[which, k],
                    partner,
                )
            )

    grads = [(combine_out_ref[:, r : r + 1] * padded[...]).astype(bf16) for r in range(2)]
    grad_copies, grad_shared = send_chunks(
        lambda slots: sum(mxu(one_hot(target_t_ref[r : r + 1] == slots), grads[r]) for r in range(2)),
        grad_chunks,
        grad_arrived_ref,
        0,
    )
    for which in range(2):
        loads[which].wait()
        for tile in range(width // LANES):
            pair = [unpick(which, tile, e) for e in range(EXP_DEV)]
            lanes = slice(tile * LANES, (tile + 1) * LANES)
            for j in range(EXP_DEV):
                expert_shard[EXP_DEV * which + j, :, lanes] = jnp.where(
                    core == 0, pair[j], pair[1 - j]
                )
    spread_rows(tokens_ref[...].astype(jnp.float32), padded)
    normed, unused, unused = layer_norm(padded[...], gains_ref[0:1], biases_ref[0:1])
    normed_low = normed.astype(bf16)
    weights = [
        remote(
            expert_shard,
            expert_w_ref.at[:, here, :],
            expert_send.at[k - 1],
            expert_recv.at[k - 1],
            {"dp": peer(dp_here, k)},
        )
        for k in (1, 2)
    ]
    kept.append(keep(expert_shard, expert_w_ref.at[:, here, :], keep_sems.at[0]))
    for which in range(2):
        loads[2 + which].wait()
        for tile in range(width // LANES):
            for e in range(EXP_DEV):
                moment_shard[EXP_DEV * which + e, :, tile * LANES : (tile + 1) * LANES] = unpick(
                    2 + which, tile, e
                )
    for copy in inner:
        copy.wait_recv()
    qkv_ref[...] = mxu(normed_low, weight_ref[:, :qcols]).astype(bf16)
    gift_ref[0:D, :] = weight_ref[:, qcols:]
    attend(qkv_ref, probs_ref, gift_ref)
    gift = remote(gift_ref, gift_other_ref, gift_sems.at[0], gift_sems.at[1], partner)
    half = padded[...] + mxu(gift_ref[D:, :], gift_ref[0:D, :], NT)
    gift.wait()
    state = half + mxu(gift_other_ref[D:, :], gift_other_ref[0:D, :], NT)
    state_ref[...] = state
    normed, unused, unused = layer_norm(state, gains_ref[1:2], biases_ref[1:2])
    normed_low = normed.astype(bf16)
    token_copies, token_shared = send_chunks(
        lambda slots: mxu(
            one_hot((target_t_ref[0:1] == slots) | (target_t_ref[1:2] == slots)), normed_low
        ),
        token_chunks,
        arrived_ref,
        1,
    )
    for copy in weights:
        copy.wait_recv()
    for k, part in ((1, slice(0, EXP_DEV)), (2, slice(EXP_DEV, 2 * EXP_DEV))):
        block = expert_w_ref.at[part, block_rows(peer(dp_here, k), shard_rows), :]
        weights.append(
            remote(
                block,
                block,
                expert_send.at[k + 1],
                expert_recv.at[k + 1],
                {"dp": peer(dp_here, 3 - k)},
            )
        )
    share_arrivals(grad_copies, grad_arrived_ref, 0, grad_shared)
    share_arrivals(token_copies, arrived_ref, 1, token_shared)
    for copy in grad_shared + token_shared + weights[2:]:
        copy.wait()
    for copy in weights[:2] + inner:
        copy.wait_send()
    for copies in (grad_copies, token_copies):
        for k in PAIRS:
            copies[k].wait_send()
    for copy in kept:
        copy.wait()


def back_kernel(
    combine_ref,
    target_ref,
    gains_ref,
    biases_ref,
    inward_moment_ref,
    outward_moment_ref,
    cot_hbm,
    tokens_hbm,
    state_hbm,
    gift_hbm,
    qkv_hbm,
    probs_hbm,
    weight_hbm,
    expert_w_hbm,
    arrived_hbm,
    grad_arrived_hbm,
    moment_hbm,
    input_ref,
    block_ref,
    norm_ref,
    attend_grad_ref,
    attend_whole_ref,
    own_steps_ref,
    home_grads_ref,
    give,
    handed,
    summed,
    returned,
    matrices,
    near_in,
    far_out,
    far_in,
    moment_whole,
    owned_low,
    normed_part,
    normed_other,
    inner,
    inner_in,
    plane,
    quarter_in,
    quarter,
    plane_total,
    whole_own,
    norm_own,
    norm_in,
    gram,
    gram_other,
    hand_send,
    hand_recv,
    slot_send,
    slot_recv,
    share_send,
    share_recv,
    pair_send,
    pair_recv,
    dp_send,
    dp_recv,
    expert_send,
    expert_recv,
    near_send,
    near_recv,
    far_send,
    far_recv,
    own_sems,
    load_sems,
):
    bf16, f32 = jnp.bfloat16, jnp.float32
    dp_here, expert_here, core = (lax.axis_index(a) for a in ("dp", "expert", "tensor"))
    partner = {"tensor": 1 - core}
    capacity = give.shape[2]
    shard_rows = inner.shape[1]
    here = block_rows(dp_here, shard_rows)
    ready = greet(dp_here, expert_here, core)
    sent = []

    def to_dp(stage, sources, targets, peers=PAIRS):
        def copy(k):
            return Copy(
                lambda: (
                    sources(k),
                    targets(k),
                    dp_send.at[stage, k - 1],
                    dp_recv.at[stage, k - 1],
                    {"dp": peer(dp_here, k)},
                )
            )

        copies = [copy(k) for k in peers]
        sent.extend(copies)
        return copies

    def to_expert(stage, sources, targets):
        def copy(k):
            return Copy(
                lambda: (
                    sources(k),
                    targets(k),
                    expert_send.at[stage, k - 1],
                    expert_recv.at[stage, k - 1],
                    {"expert": peer(expert_here, k)},
                )
            )

        copies = [copy(k) for k in PAIRS]
        sent.extend(copies)
        return copies

    def arrive(copies):
        for copy in copies:
            copy.wait_recv()

    shares = ([], [])

    def hand(which, k, start=True):
        return Copy(
            lambda: (
                give.at[which, k],
                handed.at[which, k],
                hand_send.at[which, k],
                hand_recv.at[which, k],
                partner,
            ),
            start,
        )

    def add_up(which, k):
        hand(which, k, start=False).wait_recv()
        total = (summed[which, k].astype(f32) + handed[which, k].astype(f32)).astype(bf16)
        summed[which, k] = total

    def send_home(which, k, start=True):
        return Copy(
            lambda: (
                summed.at[which, k],
                returned.at[which, 0, k],
                slot_send.at[which, k],
                slot_recv.at[which, k],
                {"expert": peer(expert_here, k)},
            ),
            start,
        )

    def stay_home(which):
        returned[which, 0, 0] = summed[which, 0]
        shares[which].append(
            Copy(
                lambda: (
                    summed.at[which, 0],
                    returned.at[which, 1, 0],
                    share_send.at[which, 0],
                    share_recv.at[which, 0],
                    partner,
                )
            )
        )

    def share(which):
        def copy(k):
            return Copy(
                lambda: (
                    returned.at[which, 0, k],
                    returned.at[which, 1, k],
                    share_send.at[which, k],
                    share_recv.at[which, k],
                    partner,
                )
            )

        for k in FAR_FIRST[:3]:
            send_home(which, k, start=False).wait_recv()
            shares[which].append(copy(k))
        sent.extend(shares[which])
        arrive(shares[which])

    def held(index):
        return 2 * (index // 2) + (index % 2 + core) % 2

    ways = ((slice(0, D // 2), 1, 2), (slice(D // 2, D), 2, 1))

    def near_copy(half, place):
        rows, first, second = ways[half]
        owner = (first, 3)[place]
        return Copy(
            lambda: (
                matrices.at[held(peer(dp_here, owner)), rows, :],
                near_in.at[half, place],
                near_send.at[half, place],
                near_recv.at[half, place],
                {"dp": peer(dp_here, first)},
            )
        )

    def far_copy(half):
        rows, first, second = ways[half]
        return Copy(
            lambda: (
                far_out.at[half],
                far_in.at[half],
                far_send.at[half],
                far_recv.at[half],
                {"dp": peer(dp_here, second)},
            )
        )

    def pass_on(near):
        arrive(near)
        for half, (rows, first, second) in enumerate(ways):
            far_out[half] = (
                matrices[held(peer(dp_here, second)), rows, :].astype(f32)
                + near_in[half, 1].astype(f32)
            ).astype(bf16)
        far = [far_copy(half) for half in range(2)]
        sent.extend(far)
        return far

    def experts(weights, rows, grads, hidden, pre_grad):
        loads = {}
        for j in (1, 0):
            for place, (source, target) in enumerate(
                (
                    (expert_w_hbm.at[j], weights.at[j]),
                    (arrived_hbm.at[j], rows.at[j]),
                    (expert_w_hbm.at[EXP_DEV + j], weights.at[EXP_DEV + j]),
                    (grad_arrived_hbm.at[j], grads.at[j]),
                )
            ):
                loads[j, place] = keep(source, target, load_sems.at[4 * j + place])
        ready()
        moments.extend(
            to_dp(0, lambda k: moment_hbm.at[peer(dp_here, k)], lambda k: moment_whole.at[here, :])
        )

        def chunk(k, first=False):
            for j in (1, 0):
                if first:
                    loads[j, 0].wait()
                    loads[j, 1].wait()
                pre = mxu(rows[j, k], weights[j])
                share_of_one = 0.5 * (1.0 + lax.erf(pre * 0.7071067811865476))
                hidden[j, k] = (pre * share_of_one).astype(bf16)
                slope = share_of_one + pre * 0.3989422804014327 * jnp.exp(-0.5 * pre * pre)
                if first:
                    loads[j, 2].wait()
                    loads[j, 3].wait()
                grad = (mxu(grads[j, k], weights[EXP_DEV + j]) * slope).astype(bf16)
                pre_grad[j, k] = grad
                entry = mxu(grad, weights[j], NT).astype(bf16)
                if j == 1:
                    give[0, k] = entry
                else:
                    summed[0, k] = entry

        def next_chunk(step, carry):
            chunk(2 - step)
            add_up(0, 3 - step)
            hand(0, 2 - step)
            send_home(0, 3 - step)
            return carry

        chunk(3, first=True)
        hand(0, 3)
        lax.fori_loop(0, 3, next_chunk, 0)

        def matrix(left, right, j):
            total = mxu(left[j, 0], right[j, 0], TN)
            for k in PAIRS:
                total += mxu(left[j, k], right[j, k], TN)
            return total.astype(bf16)

        def expert_matrices(j, carry):
            matrices[j] = matrix(rows, pre_grad, j)
            matrices[EXP_DEV + j] = matrix(grads, hidden, j)
            return carry

        lax.fori_loop(0, EXP_DEV, expert_matrices, 0)
        near = [near_copy(half, place) for place in (1, 0) for half in range(2)]
        sent.extend(near)
        add_up(0, 0)
        stay_home(0)

        def part_chunk(step, carry):
            k = 3 - step
            give[1, k] = mxu(hidden[1, k], weights[EXP_DEV + 1], NT).astype(bf16)
            summed[1, k] = mxu(hidden[0, k], weights[EXP_DEV], NT).astype(bf16)
            hand(1, k)
            return carry

        lax.fori_loop(0, 4, part_chunk, 0)
        for k in FAR_FIRST:
            add_up(1, k)
        for k in FAR_FIRST[:3]:
            send_home(1, k)
        stay_home(1)
        for which in range(2):
            sent.extend(hand(which, k, start=False) for k in range(4))
            sent.extend(send_home(which, k, start=False) for k in PAIRS)
        return near

    own_moment = keep(moment_hbm.at[dp_here], moment_whole.at[here, :], own_sems.at[0])
    near, moments = [], []
    slots = (EXP_DEV, 4, capacity)
    pl.run_scoped(
        lambda *refs: near.extend(experts(*refs)),
        pltpu.VMEM(expert_w_hbm.shape, bf16),
        pltpu.VMEM(slots + (D,), bf16),
        pltpu.VMEM(slots + (D,), bf16),
        pltpu.VMEM(slots + (expert_w_hbm.shape[2],), bf16),
        pltpu.VMEM(slots + (expert_w_hbm.shape[2],), bf16),
    )

    def backward(
        cot_ref,
        tokens_ref,
        state_ref,
        gift_ref,
        qkv_ref,
        probs_ref,
        weight_ref,
        padded,
        qkv_grad_ref,
        local_ref,
        out_grad_ref,
    ):
        loads = [
            keep(source, target, load_sems.at[place])
            for place, (source, target) in enumerate(
                (
                    (state_hbm, state_ref),
                    (cot_hbm, cot_ref),
                    (gift_hbm.at[D:, :], gift_ref),
                    (weight_hbm, weight_ref),
                    (qkv_hbm, qkv_ref),
                    (probs_hbm, probs_ref),
                    (tokens_hbm, tokens_ref),
                )
            )
        ]
        qcols = qkv_ref.shape[1]
        rows_all = state_ref.shape[0]
        loads[0].wait()
        unused, scaled2, invert2 = layer_norm(state_ref[...], gains_ref[1:2], biases_ref[1:2])
        loads[1].wait()
        spread_rows(cot_ref[...], padded)
        def pick_all(which, columns, rows):
            slot = lax.broadcasted_iota(jnp.int32, (PAD, capacity), 1)

            def picks(k, j):
                first = slot + (2 * peer(expert_here, k) + (core + j) % 2) * capacity
                hit = target_ref[rows, columns[0] : columns[0] + 1] == first
                for column in columns[1:]:
                    hit = hit | (target_ref[rows, column : column + 1] == first)
                return one_hot(hit)

            total = mxu(picks(0, 0), returned[which, 0, 0])
            for j in range(2):
                for k in FAR_FIRST:
                    if k + j > 0:
                        total += mxu(picks(k, j), returned[which, j, k])
            return total

        share(0)

        def one_gradient(image, carry):
            rows = block_rows(image, PAD)
            normed_part[rows, :] = pick_all(0, (0, 1), rows)
            return carry

        lax.fori_loop(0, rows_all // PAD, one_gradient, 0)
        normed2_grad = normed_part[...]
        norm_own[0, 4:8] = jnp.zeros((4, D), f32)
        norm_own[0, 1:2] = jnp.sum(normed2_grad * scaled2, axis=0, keepdims=True)
        norm_own[0, 3:4] = jnp.sum(normed2_grad, axis=0, keepdims=True)
        state_grad = padded[...] + norm_backward(normed2_grad, scaled2, invert2, gains_ref[1:2])
        padded[...] = state_grad
        state_low = state_grad.astype(bf16)
        for copy in loads[2:]:
            copy.wait()

        local_ref[:, qcols:] = mxu(state_low, gift_ref[...], TN)
        out_grad_ref[...] = mxu(state_low, weight_ref[:, qcols:]).astype(bf16)
        heads_here = qcols // (3 * HD)
        scale = HD ** (-0.5)

        def one_image(image, carry):
            rows = block_rows(image, PAD)
            for head in range(heads_here):
                base = head * 3 * HD
                query = qkv_ref[rows, base : base + HD]
                key = qkv_ref[rows, base + HD : base + 2 * HD]
                value = qkv_ref[rows, base + 2 * HD : base + 3 * HD]
                out_grad = out_grad_ref[rows, head * HD : (head + 1) * HD]
                probs = probs_ref[image * heads_here + head]
                prob_grad = mxu(out_grad, value, NT)
                score_grad = (
                    probs * (prob_grad - jnp.sum(probs * prob_grad, axis=-1, keepdims=True))
                ).astype(bf16)
                qkv_grad_ref[rows, base : base + HD] = (mxu(score_grad, key) * scale).astype(bf16)
                qkv_grad_ref[rows, base + HD : base + 2 * HD] = (
                    mxu(score_grad, query, TN) * scale
                ).astype(bf16)
                qkv_grad_ref[rows, base + 2 * HD : base + 3 * HD] = mxu(
                    probs.astype(bf16), out_grad, TN
                ).astype(bf16)
            return carry

        lax.fori_loop(0, rows_all // PAD, one_image, 0)
        spread_rows(tokens_ref[...].astype(f32), normed_part)
        normed1, scaled1, invert1 = layer_norm(normed_part[...], gains_ref[0:1], biases_ref[0:1])
        local_ref[:, :qcols] = mxu(normed1.astype(bf16), qkv_grad_ref[...], TN)
        for k in range(4):
            inner[k] = local_ref[block_rows(peer(dp_here, k), shard_rows), :].astype(bf16)
        normed_part[...] = mxu(qkv_grad_ref[...], weight_ref[:, :qcols], NT)
        rows_sums = to_dp(1, lambda k: inner.at[k], lambda k: inner_in.at[k - 1])
        pair = Copy(
            lambda: (normed_part, normed_other, pair_send.at[0], pair_recv.at[0], partner)
        )
        sent.append(pair)
        far = pass_on(near)

        share(1)

        def one_output(image, carry):
            rows = block_rows(image, PAD)
            total = state_ref[rows, :]
            for r in range(2):
                total += combine_ref[rows, r : r + 1] * pick_all(1, (r,), rows)
            state_ref[rows, :] = total
            return carry

        lax.fori_loop(0, rows_all // PAD, one_output, 0)
        gather_rows(state_ref[...], block_ref)

        pair.wait_recv()
        normed1_grad = normed_part[...] + normed_other[...]
        norm_own[0, 0:1] = jnp.sum(normed1_grad * scaled1, axis=0, keepdims=True)
        norm_own[0, 2:3] = jnp.sum(normed1_grad, axis=0, keepdims=True)
        norm_in[0, dp_here] = norm_own[0]
        norms = to_dp(2, lambda k: norm_own.at[0], lambda k: norm_in.at[0, dp_here])
        gather_rows(
            padded[...] + norm_backward(normed1_grad, scaled1, invert1, gains_ref[0:1]), input_ref
        )
        return rows_sums, norms, far

    travelling = []
    rows_f32 = pltpu.VMEM(state_hbm.shape, f32)
    pl.run_scoped(
        lambda *refs: travelling.extend(backward(*refs)),
        pltpu.VMEM(cot_hbm.shape, f32),
        pltpu.VMEM(tokens_hbm.shape, bf16),
        rows_f32,
        pltpu.VMEM((gift_hbm.shape[0] - D, gift_hbm.shape[1]), bf16),
        pltpu.VMEM(qkv_hbm.shape, bf16),
        pltpu.VMEM(probs_hbm.shape, f32),
        pltpu.VMEM(weight_hbm.shape, bf16),
        rows_f32,
        pltpu.VMEM(qkv_hbm.shape, bf16),
        pltpu.VMEM(weight_hbm.shape, f32),
        pltpu.VMEM((state_hbm.shape[0], gift_hbm.shape[1]), bf16),
    )
    rows_sums, norms, far = travelling

    arrive(rows_sums)
    plane[...] = (
        inner[0].astype(f32)
        + inner_in[0].astype(f32)
        + inner_in[1].astype(f32)
        + inner_in[2].astype(f32)
    ).astype(bf16)
    quarter_rows = quarter.shape[0]
    my_quarter = block_rows(expert_here, quarter_rows)
    quarters = to_expert(
        0,
        lambda k: plane.at[block_rows(peer(expert_here, k), quarter_rows), :],
        lambda k: quarter_in.at[k - 1],
    )
    arrive(norms)
    norm_plane = norm_in[0, 0] + norm_in[0, 1] + norm_in[0, 2] + norm_in[0, 3]
    norm_own[1] = norm_plane
    norm_in[1, expert_here] = norm_plane
    norm_sums = to_expert(1, lambda k: norm_own.at[1], lambda k: norm_in.at[1, expert_here])

    def orthogonalize(owned_next, factor, change):
        arrive(quarters)
        quarter[...] = (
            plane[my_quarter, :].astype(f32)
            + quarter_in[0].astype(f32)
            + quarter_in[1].astype(f32)
            + quarter_in[2].astype(f32)
        ).astype(bf16)
        plane_total[my_quarter, :] = quarter[...]
        totals = to_expert(2, lambda k: quarter, lambda k: plane_total.at[my_quarter, :])
        arrive(far + moments)
        own_moment.wait()
        for half, (rows, first, second) in enumerate(ways):
            owned = (
                matrices[held(dp_here), rows, :].astype(f32)
                + near_in[half, 0].astype(f32)
                + far_in[half].astype(f32)
            )
            owned_low[rows, :] = owned.astype(bf16)
            owned_next[rows, :] = 0.95 * moment_whole[rows, :].astype(f32) + owned
        split = halves(owned_next[...])
        gram[...] = mxu3(split, split, NT)
        pair = remote(gram, gram_other, pair_send.at[1], pair_recv.at[1], partner)
        home = to_dp(
            3,
            lambda k: owned_low.at[block_rows(peer(dp_here, k), shard_rows), :],
            lambda k: home_grads_ref.at[dp_here],
        )
        own = keep(owned_low.at[here, :], home_grads_ref.at[dp_here], load_sems.at[1])
        pair.wait()

        def attention_next():
            arrive(totals)
            total = plane_total[...].astype(f32)
            attend_grad_ref[...] = total
            qcols = inward_moment_ref.shape[1]
            whole_own[:, :qcols] = (0.95 * inward_moment_ref[...] + total[:, :qcols]).astype(bf16)
            whole_own[:, qcols:] = (0.95 * outward_moment_ref[...] + total[:, qcols:]).astype(bf16)
            attend_whole_ref[here, :] = whole_own[...]
            wholes.extend(to_dp(4, lambda k: whole_own, lambda k: attend_whole_ref.at[here, :]))

        wholes = []
        find_factor(gram[...] + gram_other[...], factor, gram, change, gram_other, attention_next)
        own_steps_ref[...] = (
            mxu3(halves(factor[...]), halves(owned_next[...])) * (0.2 * math.sqrt(F))
        ).astype(bf16)
        arrive(norm_sums)
        norm_ref[...] = (
            norm_in[1, 0, 0:4] + norm_in[1, 1, 0:4] + norm_in[1, 2, 0:4] + norm_in[1, 3, 0:4]
        )
        arrive(home)
        arrive(wholes)
        own.wait()

    square = pltpu.VMEM((D, D), f32)
    pl.run_scoped(orthogonalize, pltpu.VMEM(moment_whole.shape, f32), square, square)
    for copy in sent:
        copy.wait_send()


def halves(value):
    high = value.astype(jnp.bfloat16)
    return high, (value - high.astype(jnp.float32)).astype(jnp.bfloat16)


def mxu3(left, right, dims=(((1,), (0,)), ((), ()))):
    return (
        mxu(left[0], right[0], dims) + mxu(left[1], right[0], dims) + mxu(left[0], right[1], dims)
    )


def find_factor(gram, factor, current, change, scaled, between=None):
    diagonal = lax.broadcasted_iota(jnp.int32, gram.shape, 0) == lax.broadcasted_iota(
        jnp.int32, gram.shape, 1
    )
    squares = jnp.sum(
        jnp.sum(jnp.where(diagonal, gram, 0.0), axis=1, keepdims=True), axis=0, keepdims=True
    )
    norm = jnp.sqrt(squares) + 1e-07
    current[...] = gram / (norm * norm)
    factor[...] = jnp.where(diagonal, 1.0 / norm, 0.0)
    half = D // 2

    def stacked(left, right):
        count = left[0].shape[0]
        both = mxu(jnp.concatenate(left, axis=0), right[0])
        return both[:count] + both[count:] + mxu(left[0], right[1])

    def product(out, left, right, by, added, added_by):
        first = stacked(left, [x[:, :half] for x in right])
        first = by * first + added_by * added[:, :half]
        corner = stacked([x[half:] for x in left], [x[:, half:] for x in right])
        corner = by * corner + added_by * added[half:, half:]
        out[:, :half] = first
        out[:half, half:] = first[half:].T
        out[half:, half:] = corner

    def sweep(index, carry):
        if between is not None:
            pl.when(index == MIDWAY)(between)
        low = halves(current[...])
        product(change, low, low, 2.0315, current, -4.775)
        step = halves(change[...])
        product(factor, step, halves(factor[...]), 1.0, factor, 3.4445)

        @pl.when(index < 4)
        def next_gram():
            product(scaled, step, low, 1.0, current, 3.4445)
            product(current, halves(scaled[...]), step, 1.0, scaled, 3.4445)

        return carry

    lax.fori_loop(0, 5, sweep, 0)


def finish_kernel(
    whole_ref,
    own_steps_ref,
    home_steps_ref,
    attend_step_ref,
    kept,
    given,
    taken,
    factor,
    change,
    mine,
    other,
    step_send,
    step_recv,
    pair_send,
    pair_recv,
):
    dp_here, core = lax.axis_index("dp"), lax.axis_index("tensor")
    partner = {"tensor": 1 - core}
    shard_rows = mine.shape[0]
    qcols = 3 * whole_ref.shape[1] // 4
    here = block_rows(dp_here, shard_rows)
    ready = greet(dp_here, None, core, over_expert=False)
    inward_gram = mxu(whole_ref[:, :qcols], whole_ref[:, :qcols], NT)
    outward_gram = mxu(whole_ref[:, qcols:], whole_ref[:, qcols:], NT)
    kept[...] = jnp.where(core == 0, inward_gram, outward_gram)
    given[...] = jnp.where(core == 0, outward_gram, inward_gram)
    ready()
    pair = remote(given, taken, pair_send.at[0], pair_recv.at[0], partner)
    steps = [
        remote(
            own_steps_ref.at[block_rows(peer(dp_here, k), shard_rows), :],
            home_steps_ref.at[dp_here],
            step_send.at[k - 1],
            step_recv.at[k - 1],
            {"dp": peer(dp_here, k)},
        )
        for k in PAIRS
    ]
    home_steps_ref[dp_here] = own_steps_ref[here, :]
    pair.wait()
    find_factor(kept[...] + taken[...], factor, kept, change, taken)
    mine[...] = factor[here, :]
    pair = remote(mine, other, pair_send.at[1], pair_recv.at[1], partner)
    for copy in steps:
        copy.wait()
    pair.wait()
    for owner, columns, count in ((0, slice(0, qcols), 3 * D), (1, slice(qcols, None), D)):
        rows = halves(jnp.where(core == owner, mine[...], other[...]))
        step = mxu(rows[0], whole_ref[:, columns]) + mxu(rows[1], whole_ref[:, columns])
        attend_step_ref[:, columns] = step * (0.2 * math.sqrt(count))


def apply_kernel(
    steps_done_ref,
    home_steps_ref,
    attend_step_ref,
    home_grads_ref,
    attend_grad_ref,
    norm_ref,
    gains_ref,
    biases_ref,
    first_ref,
    second_ref,
    inward_ref,
    outward_ref,
    up_ref,
    down_ref,
    inward_moment_ref,
    outward_moment_ref,
    up_moment_ref,
    down_moment_ref,
    block_ref,
    input_ref,
    block_out_ref,
    input_out_ref,
    inward_gradient_ref,
    outward_gradient_ref,
    up_gradient_ref,
    down_gradient_ref,
    gain_gradient_ref,
    bias_gradient_ref,
    inward_next_ref,
    outward_next_ref,
    up_next_ref,
    down_next_ref,
    inward_new_ref,
    outward_new_ref,
    up_new_ref,
    down_new_ref,
    inward_copy_ref,
    outward_copy_ref,
    up_copy_ref,
    down_copy_ref,
    gains_new_ref,
    biases_new_ref,
    first_new_ref,
    second_new_ref,
    weave,
):
    f32 = jnp.float32
    qcols = inward_ref.shape[1]
    block_out_ref[...] = block_ref[...]
    input_out_ref[...] = input_ref[...]

    def finish(place, gradient, step, refs):
        master_ref, moment_ref, gradient_ref, next_ref, new_ref, copy_ref = refs
        gradient_ref[place] = gradient
        next_ref[place] = 0.95 * moment_ref[place] + gradient
        master = master_ref[place]
        new = master - 0.1 * (step + 0.1 * master)
        new_ref[place] = new
        copy_ref[place] = new.astype(copy_ref.dtype)

    experts = (
        (up_ref, up_moment_ref, up_gradient_ref, up_next_ref, up_new_ref, up_copy_ref),
        (down_ref, down_moment_ref, down_gradient_ref, down_next_ref, down_new_ref, down_copy_ref),
    )
    everything = (slice(None), slice(None))
    rows, width = attend_grad_ref.shape
    for which, refs in enumerate(experts):
        for place, home_ref in enumerate((home_grads_ref, home_steps_ref)):
            for e in range(EXP_DEV):
                for tile in range(width // LANES):
                    weave[place, strand(tile, e, rows, width), :] = home_ref[
                        EXP_DEV * which + e, :, tile * LANES : (tile + 1) * LANES
                    ].astype(f32)
        finish(everything, weave[0], weave[1], refs)
    finish(
        everything,
        attend_grad_ref[:, :qcols],
        attend_step_ref[:, :qcols],
        (
            inward_ref,
            inward_moment_ref,
            inward_gradient_ref,
            inward_next_ref,
            inward_new_ref,
            inward_copy_ref,
        ),
    )
    finish(
        everything,
        attend_grad_ref[:, qcols:],
        attend_step_ref[:, qcols:],
        (
            outward_ref,
            outward_moment_ref,
            outward_gradient_ref,
            outward_next_ref,
            outward_new_ref,
            outward_copy_ref,
        ),
    )

    @pl.when(pl.program_id(0) == 0)
    def norms():
        total = norm_ref[...]
        gain_gradient_ref[...] = total[0:2]
        bias_gradient_ref[...] = total[2:4]
        moment_first = 0.9 * first_ref[...] + 0.1 * total
        moment_second = 0.999 * second_ref[...] + 0.001 * total * total
        first_new_ref[...] = moment_first
        second_new_ref[...] = moment_second
        done = jnp.full((4, D), steps_done_ref[0], jnp.int32).astype(f32)
        direction = (
            moment_first
            / (1.0 - jnp.power(0.9, done))
            / (jnp.sqrt(moment_second / (1.0 - jnp.power(0.999, done))) + 1e-08)
        )
        gains_new_ref[...] = gains_ref[...] - 0.1 * direction[0:2]
        biases_new_ref[...] = biases_ref[...] - 0.1 * direction[2:4]


def pair_body(
    tokens_in,
    expert_ids,
    combine,
    out_cot,
    inward_master,
    outward_master,
    up_master,
    down_master,
    norm_gains,
    norm_biases,
    inward_moment,
    outward_moment,
    up_moment,
    down_moment,
    first_moment,
    second_moment,
    step_count,
):
    bf16, f32 = jnp.bfloat16, jnp.float32
    token_rows = tokens_in.shape[0]
    expert_total = EXP_DEV * 4
    capacity = (token_rows * 10 // (4 * expert_total) + 7) // 8 * 8
    shard_rows, qcols = inward_master.shape
    width = up_master.shape[2]
    images = token_rows // SEQ
    padded_rows = images * PAD
    heads_here = qcols // (3 * HD)
    shape = jax.ShapeDtypeStruct
    rows_f32 = pltpu.VMEM((padded_rows, D), f32)
    in_vmem, anywhere = pl.BlockSpec(memory_space=pltpu.VMEM), pl.BlockSpec(memory_space=pl.ANY)
    dma = pltpu.SemaphoreType.DMA

    slots = shape((EXP_DEV, 4, capacity, D), bf16)
    (
        state,
        gift,
        qkv_low,
        probs,
        weight,
        target,
        combine_padded,
        moment_shard,
        expert_w,
        arrived,
        grad_arrived,
    ) = pl.pallas_call(
        front_kernel,
        out_shape=(
            shape((padded_rows, D), f32),
            shape((D + padded_rows, heads_here * HD), bf16),
            shape((padded_rows, qcols), bf16),
            shape((images * heads_here, PAD, PAD), f32),
            shape((D, width), bf16),
            shape((padded_rows, 128), jnp.int32),
            shape((padded_rows, 2), f32),
            shape((4, shard_rows, width), bf16),
            shape((2 * EXP_DEV, D, width), bf16),
            slots,
            slots,
        ),
        in_specs=[in_vmem] * 8 + [anywhere] * 4,
        out_specs=tuple([in_vmem] * 8 + [anywhere] * 3),
        scratch_shapes=[
            rows_f32,
            pltpu.VMEM((8, token_rows), f32),
            pltpu.VMEM((padded_rows, 128), f32),
            pltpu.VMEM((4, EXP_DEV * shard_rows * width // LANES, LANES), f32),
            pltpu.VMEM((2, padded_rows), jnp.int32),
            pltpu.VMEM((shard_rows, width), bf16),
            pltpu.VMEM((4, shard_rows, width), bf16),
            pltpu.VMEM((D + padded_rows, heads_here * HD), bf16),
            pltpu.VMEM((4, capacity, D), bf16),
            pltpu.VMEM((4, capacity, D), bf16),
            dma((3,)),
            dma((3,)),
            dma((4,)),
            dma((4,)),
            dma((2, 4)),
            dma((2, 4)),
            dma((2, 4)),
            dma((2, 4)),
            dma((2,)),
            dma((3,)),
            dma((4,)),
        ],
        name="front",
        cost_estimate=pl.CostEstimate(
            flops=60_000_000_000, bytes_accessed=30_000_000, transcendentals=0
        ),
        compiler_params=pltpu.CompilerParams(collective_id=0, has_side_effects=True),
    )(
        expert_ids.T,
        combine.T,
        out_cot,
        tokens_in,
        norm_gains,
        norm_biases,
        inward_master,
        outward_master,
        *(woven(a) for a in (up_master, down_master, up_moment, down_moment)),
    )
    chunks = (2, 4, capacity, D)
    square = pltpu.VMEM((D, D), f32)
    rows_low = pltpu.VMEM((shard_rows, width), bf16)
    (
        input_gradient,
        block_out,
        norm_total,
        attend_grad,
        attend_whole,
        own_steps,
        home_grads,
    ) = pl.pallas_call(
        back_kernel,
        out_shape=(
            shape((token_rows, D), f32),
            shape((token_rows, D), bf16),
            shape((4, D), f32),
            shape((shard_rows, width), f32),
            shape((D, width), bf16),
            shape((D, width), bf16),
            shape((4, shard_rows, width), bf16),
        ),
        in_specs=[in_vmem] * 6 + [anywhere] * 11,
        out_specs=tuple([in_vmem] * 6 + [anywhere]),
        scratch_shapes=[
            pltpu.VMEM(chunks, bf16),
            pltpu.VMEM(chunks, bf16),
            pltpu.VMEM(chunks, bf16),
            pltpu.VMEM((2,) + chunks, bf16),
            pltpu.VMEM((4, D, width), bf16),
            pltpu.VMEM((2, 2, D // 2, width), bf16),
            pltpu.VMEM((2, D // 2, width), bf16),
            pltpu.VMEM((2, D // 2, width), bf16),
            pltpu.VMEM((D, width), bf16),
            pltpu.VMEM((D, width), bf16),
            rows_f32,
            rows_f32,
            pltpu.VMEM((4, shard_rows, width), bf16),
            pltpu.VMEM((3, shard_rows, width), bf16),
            rows_low,
            pltpu.VMEM((3, shard_rows // 4, width), bf16),
            pltpu.VMEM((shard_rows // 4, width), bf16),
            rows_low,
            rows_low,
            pltpu.VMEM((2, 8, D), f32),
            pltpu.VMEM((2, 4, 8, D), f32),
            square,
            square,
        ]
        + [dma((2, 4))] * 6
        + [dma((2,))] * 2
        + [dma((5, 3))] * 2
        + [dma((3, 3))] * 2
        + [dma((2, 2))] * 2
        + [dma((2,))] * 2
        + [dma((1,))]
        + [dma((8,))],
        name="back",
        cost_estimate=pl.CostEstimate(
            flops=110_000_000_000, bytes_accessed=60_000_000, transcendentals=0
        ),
        compiler_params=pltpu.CompilerParams(
            collective_id=1, has_side_effects=True, vmem_limit_bytes=66_000_000
        ),
    )(
        combine_padded,
        target,
        norm_gains,
        norm_biases,
        inward_moment,
        outward_moment,
        out_cot,
        tokens_in,
        state,
        gift,
        qkv_low,
        probs,
        weight,
        expert_w,
        arrived,
        grad_arrived,
        moment_shard,
    )
    factor_rows = pltpu.VMEM((shard_rows, D), f32)
    home_steps, attend_step = pl.pallas_call(
        finish_kernel,
        out_shape=(shape((4, shard_rows, width), bf16), shape((shard_rows, width), f32)),
        in_specs=[in_vmem] * 2,
        out_specs=(in_vmem, in_vmem),
        scratch_shapes=[square] * 5 + [factor_rows] * 2 + [dma((3,))] * 2 + [dma((2,))] * 2,
        name="finish",
        cost_estimate=pl.CostEstimate(
            flops=20_000_000_000, bytes_accessed=5_000_000, transcendentals=0
        ),
        compiler_params=pltpu.CompilerParams(collective_id=2, has_side_effects=True),
    )(attend_whole, own_steps)

    blocks = 4
    inward, outward = inward_master.shape, outward_master.shape
    expert = (EXP_DEV * shard_rows * width // LANES, LANES)

    def split(whole, along=0):
        if along is None:
            return pl.BlockSpec(whole, lambda i: (0,) * len(whole))
        rows = pl.cdiv(pl.cdiv(whole[along], blocks), 8) * 8
        block = whole[:along] + (rows,) + whole[along + 1 :]
        return pl.BlockSpec(
            block, lambda i: (0,) * along + (i,) + (0,) * (len(whole) - along - 1)
        )

    two, four, attended = (2, D), (4, D), (shard_rows, width)
    matrix_shapes = (inward, outward, expert, expert)
    by_rows = [split(m) for m in matrix_shapes]
    tokens = split((token_rows, D))
    finished = pl.pallas_call(
        apply_kernel,
        grid=(blocks,),
        out_shape=tuple(
            [shape((token_rows, D), bf16), shape((token_rows, D), f32)]
            + [shape(m, f32) for m in matrix_shapes]
            + [shape(two, f32)] * 2
            + [shape(m, f32) for m in matrix_shapes * 2]
            + [shape(m, bf16) for m in matrix_shapes]
            + [shape(two, f32)] * 2
            + [shape(four, f32)] * 2
        ),
        in_specs=[pl.BlockSpec(memory_space=pltpu.SMEM)]
        + [split((4,) + attended, 1), split(attended), split((4,) + attended, 1), split(attended)]
        + [split(four, None), split(two, None), split(two, None), split(four, None), split(four, None)]
        + by_rows * 2
        + [tokens] * 2,
        out_specs=tuple(
            [tokens] * 2
            + by_rows
            + [split(two, None)] * 2
            + by_rows * 3
            + [split(two, None)] * 2
            + [split(four, None)] * 2
        ),
        scratch_shapes=[pltpu.VMEM((2, expert[0] // blocks, LANES), f32)],
        name="apply",
        cost_estimate=pl.CostEstimate(
            flops=20_000_000, bytes_accessed=20_000_000, transcendentals=0
        ),
    )(
        step_count,
        home_steps,
        attend_step,
        home_grads,
        attend_grad,
        norm_total,
        norm_gains,
        norm_biases,
        first_moment,
        second_moment,
        inward_master,
        outward_master,
        woven(up_master),
        woven(down_master),
        inward_moment,
        outward_moment,
        woven(up_moment),
        woven(down_moment),
        block_out,
        input_gradient,
    )
    return tuple(
        unwoven(a, up_master.shape) if a.shape == expert else a for a in finished
    )


def solution(mesh):
    sizes = tuple(mesh.shape[axis] for axis in ("dp", "expert", "tensor"))
    body = pair_body if sizes == (4, 4, 2) else start_body
    return jax.shard_map(
        body,
        mesh=mesh,
        in_specs=(
            P(("dp", "expert"), None),
            P(("dp", "expert"), None),
            P(("dp", "expert"), None),
            P(("dp", "expert"), None),
            P("dp", "tensor"),
            P("dp", "tensor"),
            P("dp", "expert", "tensor"),
            P("dp", "expert", "tensor"),
            P(),
            P(),
            P("dp", "tensor"),
            P("dp", "tensor"),
            P("dp", "expert", "tensor"),
            P("dp", "expert", "tensor"),
            P(),
            P(),
            P(),
        ),
        out_specs=(
            P(("dp", "expert"), None),
            P(("dp", "expert"), None),
            P("dp", "tensor"),
            P("dp", "tensor"),
            P("dp", "expert", "tensor"),
            P("dp", "expert", "tensor"),
            P(),
            P(),
            P("dp", "tensor"),
            P("dp", "tensor"),
            P("dp", "expert", "tensor"),
            P("dp", "expert", "tensor"),
            P("dp", "tensor"),
            P("dp", "tensor"),
            P("dp", "expert", "tensor"),
            P("dp", "expert", "tensor"),
            P("dp", "tensor"),
            P("dp", "tensor"),
            P("dp", "expert", "tensor"),
            P("dp", "expert", "tensor"),
            P(),
            P(),
            P(),
            P(),
        ),
        check_vma=False,
    )
```

profile of v0, /device:TPU:0, one launch (start us, length us, event | category | flops | bytes accessed | tf_op | source)
XLA Modules:
  0.0 212.7 jit_solution(16274519827002978906)
XLA Ops:
  0.7 62.7 %front.1 = (f32[832,512]{1,0:T(8,128)}, bf16[1344,256]{1,0:T(8,128)(2,1)}, bf16[832,768]{1,0:T(8,128)(2,1)}, f32[16,208,208]{2,1,0:T(8,128)}, bf16[512,1024]{1,0...) custom-call(s32[2,788]{1,0:T(2,128)} %bitcast.78, ...), custom_call_target="tpu_custom_call" | custom-call | flops 60000002048 | bytes 30000000 | tf_op jit(solution)/shard_map/front/pallas_call | solution.py:1550
  63.4 113.2 %back.1 = (f32[788,512]{1,0:T(8,128)}, bf16[788,512]{1,0:T(8,128)(2,1)}, f32[4,512]{1,0:T(4,128)}, f32[128,1024]{1,0:T(8,128)}, bf16[512,1024]{1,0:T(8,128)(2,1)...) custom-call(f32[832,2]{1,0:T(8,128)} %get-tuple-element.68.combine_ref, ...), custom_call_target="tpu_custom_call" | custom-call | flops 109999996928 | bytes 60000000 | tf_op jit(solution)/shard_map/back/pallas_call | solution.py:1617
  176.6 25.4 %finish.1 = (bf16[4,128,1024]{2,1,0:T(8,128)(2,1)}, f32[128,1024]{1,0:T(8,128)}) custom-call(bf16[512,1024]{1,0:T(8,128)(2,1)} %get-tuple-element.79.whole_ref, bf16[512,1024]{1,0:T(8,128)(2,1)} %get-tuple-element.80.own_steps_ref), custom_call_target="tpu_custom_call" | custom-call | flops 20000000000 | bytes 5000000 | tf_op jit(solution)/shard_map/finish/pallas_call | solution.py:1690
  202.7 9.8 %apply.1 = (bf16[788,512]{1,0:T(8,128)(2,1)}, f32[788,512]{1,0:T(8,128)}, f32[128,768]{1,0:T(8,128)}, f32[128,256]{1,0:T(8,128)}, f32[2048,128]{1,0:T(8,128)}, /...) custom-call(s32[1]{0:T(128)S(6)} %copy.53.steps_done_ref, ...), custom_call_target="tpu_custom_call" | custom-call | flops 20000000 | bytes 20000000 | tf_op jit(solution)/shard_map/apply/pallas_call | solution.py:1720
where the time goes:
time: 213 us
  Pallas kernels  211 us (99%)
    pallas_call x1, Pallas kernels, pair_body(): pl.pallas_call(back_kernel, out_shape=(shape((token_rows, D), f32), shape...  113 us
    pallas_call x1, Pallas kernels, pair_body(): pl.pallas_call(front_kernel, out_shape=(shape((padded_rows, D), f32), sha...  62.7 us
    pallas_call x1, Pallas kernels, pair_body(): pl.pallas_call(finish_kernel, out_shape=(shape((4, shard_rows, width), bf...  25.4 us
    pallas_call x1, Pallas kernels, pair_body(): pl.pallas_call(apply_kernel, grid=(blocks,), out_shape=tuple([shape((toke...  9.79 us

commit v1 on v0

--- a/solution.py
+++ b/solution.py
@@ -615,12 +615,15 @@
             chunks[k] = fill(slot + first_slot(k)).astype(bf16)
 
         def make_and_send(step, carry):
-            make(2 - step)
-            going(3 - step)
+            make(3 - step)
+
+            @pl.when(step > 0)
+            def send_last():
+                going(4 - step)
+
             return carry
 
-        make(3)
-        lax.fori_loop(0, 3, make_and_send, 0)
+        lax.fori_loop(0, 4, make_and_send, 0)
         copies, shared = {k: going(k, start=False) for k in PAIRS}, []
         kept.append(keep(chunks.at[0], landing.at[0, 0], keep_sems.at[1 + which]))
         shared.append(
@@ -959,22 +962,18 @@
             ):
                 loads[j, place] = keep(source, target, load_sems.at[4 * j + place])
         ready()
+        for load in loads.values():
+            load.wait()
         moments.extend(
             to_dp(0, lambda k: moment_hbm.at[peer(dp_here, k)], lambda k: moment_whole.at[here, :])
         )
 
-        def chunk(k, first=False):
+        def chunk(k):
             for j in (1, 0):
-                if first:
-                    loads[j, 0].wait()
-                    loads[j, 1].wait()
                 pre = mxu(rows[j, k], weights[j])
                 share_of_one = 0.5 * (1.0 + lax.erf(pre * 0.7071067811865476))
                 hidden[j, k] = (pre * share_of_one).astype(bf16)
                 slope = share_of_one + pre * 0.3989422804014327 * jnp.exp(-0.5 * pre * pre)
-                if first:
-                    loads[j, 2].wait()
-                    loads[j, 3].wait()
                 grad = (mxu(grads[j, k], weights[EXP_DEV + j]) * slope).astype(bf16)
                 pre_grad[j, k] = grad
                 entry = mxu(grad, weights[j], NT).astype(bf16)
@@ -984,15 +983,17 @@
                     summed[0, k] = entry
 
         def next_chunk(step, carry):
-            chunk(2 - step)
-            add_up(0, 3 - step)
-            hand(0, 2 - step)
-            send_home(0, 3 - step)
+            chunk(3 - step)
+            hand(0, 3 - step)
+
+            @pl.when(step > 0)
+            def last_chunk():
+                add_up(0, 4 - step)
+                send_home(0, 4 - step)
+
             return carry
 
-        chunk(3, first=True)
-        hand(0, 3)
-        lax.fori_loop(0, 3, next_chunk, 0)
+        lax.fori_loop(0, 4, next_chunk, 0)
 
         def matrix(left, right, j):
             total = mxu(left[j, 0], right[j, 0], TN)
@@ -1235,11 +1236,16 @@
         split = halves(owned_next[...])
         gram[...] = mxu3(split, split, NT)
         pair = remote(gram, gram_other, pair_send.at[1], pair_recv.at[1], partner)
-        home = to_dp(
-            3,
-            lambda k: owned_low.at[block_rows(peer(dp_here, k), shard_rows), :],
-            lambda k: home_grads_ref.at[dp_here],
-        )
+
+        def send_rows(peers):
+            return to_dp(
+                3,
+                lambda k: owned_low.at[block_rows(peer(dp_here, k), shard_rows), :],
+                lambda k: home_grads_ref.at[dp_here],
+                peers,
+            )
+
+        home = send_rows((1, 2))
         own = keep(owned_low.at[here, :], home_grads_ref.at[dp_here], load_sems.at[1])
         pair.wait()
 
@@ -1252,6 +1258,7 @@
             whole_own[:, qcols:] = (0.95 * outward_moment_ref[...] + total[:, qcols:]).astype(bf16)
             attend_whole_ref[here, :] = whole_own[...]
             wholes.extend(to_dp(4, lambda k: whole_own, lambda k: attend_whole_ref.at[here, :]))
+            home.extend(send_rows((3,)))
 
         wholes = []
         find_factor(gram[...] + gram_other[...], factor, gram, change, gram_other, attention_next)
@@ -1295,36 +1302,31 @@
     factor[...] = jnp.where(diagonal, 1.0 / norm, 0.0)
     half = D // 2
 
-    def stacked(left, right):
-        count = left[0].shape[0]
-        both = mxu(jnp.concatenate(left, axis=0), right[0])
-        return both[:count] + both[count:] + mxu(left[0], right[1])
-
     def product(out, left, right, by, added, added_by):
-        first = stacked(left, [x[:, :half] for x in right])
-        first = by * first + added_by * added[:, :half]
-        corner = stacked([x[half:] for x in left], [x[:, half:] for x in right])
+        upper = by * mxu3([x[:half] for x in left], right) + added_by * added[:half, :]
+        corner = mxu3([x[half:] for x in left], [x[:, half:] for x in right])
         corner = by * corner + added_by * added[half:, half:]
-        out[:, :half] = first
-        out[:half, half:] = first[half:].T
+        out[:half, :] = upper
+        out[half:, :half] = upper[:, half:].T
         out[half:, half:] = corner
 
-    def sweep(index, carry):
-        if between is not None:
-            pl.when(index == MIDWAY)(between)
+    def polynomial():
         low = halves(current[...])
         product(change, low, low, 2.0315, current, -4.775)
         step = halves(change[...])
         product(factor, step, halves(factor[...]), 1.0, factor, 3.4445)
-
-        @pl.when(index < 4)
-        def next_gram():
-            product(scaled, step, low, 1.0, current, 3.4445)
-            product(current, halves(scaled[...]), step, 1.0, scaled, 3.4445)
-
+        return low, step
+
+    def sweep(index, carry):
+        if between is not None:
+            pl.when(index == MIDWAY)(between)
+        low, step = polynomial()
+        product(scaled, step, low, 1.0, current, 3.4445)
+        product(current, halves(scaled[...]), step, 1.0, scaled, 3.4445)
         return carry
 
-    lax.fori_loop(0, 5, sweep, 0)
+    lax.fori_loop(0, 4, sweep, 0)
+    polynomial()
 
 
 def finish_kernel(

time: 213 us -> 209 us (0.981)
  Pallas kernels: 211 us -> 207 us
    pallas_call x1, Pallas kernels: 25.4 us -> 21.8 us  [pair_body(): pl.pallas_call(finish_kernel, out_shape=(shape((4, shard_rows, width), bf...]
where the time goes in v1:
time: 209 us
  Pallas kernels  207 us (99%)
    pallas_call x1, Pallas kernels, pair_body(): pl.pallas_call(back_kernel, out_shape=(shape((token_rows, D), f32), shape...  113 us
    pallas_call x1, Pallas kernels, pair_body(): pl.pallas_call(front_kernel, out_shape=(shape((padded_rows, D), f32), sha...  62.9 us
    pallas_call x1, Pallas kernels, pair_body(): pl.pallas_call(finish_kernel, out_shape=(shape((4, shard_rows, width), bf...  21.8 us
    pallas_call x1, Pallas kernels, pair_body(): pl.pallas_call(apply_kernel, grid=(blocks,), out_shape=tuple([shape((toke...  9.79 us

profile of v1, /device:TPU:0, one launch (start us, length us, event | category | flops | bytes accessed | tf_op | source)
XLA Modules:
  0.0 208.9 jit_solution(14998024441177510240)
XLA Ops:
  0.7 62.9 %front.1 = (f32[832,512]{1,0:T(8,128)}, bf16[1344,256]{1,0:T(8,128)(2,1)}, bf16[832,768]{1,0:T(8,128)(2,1)}, f32[16,208,208]{2,1,0:T(8,128)}, bf16[512,1024]{1,0...) custom-call(s32[2,788]{1,0:T(2,128)} %bitcast.78, ...), custom_call_target="tpu_custom_call" | custom-call | flops 60000002048 | bytes 30000000 | tf_op jit(solution)/shard_map/front/pallas_call | solution.py:1552
  63.6 112.9 %back.1 = (f32[788,512]{1,0:T(8,128)}, bf16[788,512]{1,0:T(8,128)(2,1)}, f32[4,512]{1,0:T(4,128)}, f32[128,1024]{1,0:T(8,128)}, bf16[512,1024]{1,0:T(8,128)(2,1)...) custom-call(f32[832,2]{1,0:T(8,128)} %get-tuple-element.68.combine_ref, ...), custom_call_target="tpu_custom_call" | custom-call | flops 109999996928 | bytes 60000000 | tf_op jit(solution)/shard_map/back/pallas_call | solution.py:1619
  176.5 21.8 %finish.1 = (bf16[4,128,1024]{2,1,0:T(8,128)(2,1)}, f32[128,1024]{1,0:T(8,128)}) custom-call(bf16[512,1024]{1,0:T(8,128)(2,1)} %get-tuple-element.79.whole_ref, bf16[512,1024]{1,0:T(8,128)(2,1)} %get-tuple-element.80.own_steps_ref), custom_call_target="tpu_custom_call" | custom-call | flops 20000000000 | bytes 5000000 | tf_op jit(solution)/shard_map/finish/pallas_call | solution.py:1692
  198.9 9.8 %apply.1 = (bf16[788,512]{1,0:T(8,128)(2,1)}, f32[788,512]{1,0:T(8,128)}, f32[128,768]{1,0:T(8,128)}, f32[128,256]{1,0:T(8,128)}, f32[2048,128]{1,0:T(8,128)}, /...) custom-call(s32[1]{0:T(128)S(6)} %copy.53.steps_done_ref, ...), custom_call_target="tpu_custom_call" | custom-call | flops 20000000 | bytes 20000000 | tf_op jit(solution)/shard_map/apply/pallas_call | solution.py:1722

commit v2 on v1

--- a/solution.py
+++ b/solution.py
@@ -772,6 +772,8 @@
     normed_other,
     inner,
     inner_in,
+    outer,
+    outer_in,
     plane,
     quarter_in,
     quarter,
@@ -906,7 +908,6 @@
             send_home(which, k, start=False).wait_recv()
             shares[which].append(copy(k))
         sent.extend(shares[which])
-        arrive(shares[which])
 
     def held(index):
         return 2 * (index // 2) + (index % 2 + core) % 2
@@ -962,18 +963,24 @@
             ):
                 loads[j, place] = keep(source, target, load_sems.at[4 * j + place])
         ready()
-        for load in loads.values():
-            load.wait()
         moments.extend(
             to_dp(0, lambda k: moment_hbm.at[peer(dp_here, k)], lambda k: moment_whole.at[here, :])
         )
 
-        def chunk(k):
+        def chunk(k, step):
+            def loaded(*places):
+                @pl.when(step == 0)
+                def wait():
+                    for place in places:
+                        loads[place].wait()
+
             for j in (1, 0):
+                loaded((j, 0), (j, 1))
                 pre = mxu(rows[j, k], weights[j])
                 share_of_one = 0.5 * (1.0 + lax.erf(pre * 0.7071067811865476))
                 hidden[j, k] = (pre * share_of_one).astype(bf16)
                 slope = share_of_one + pre * 0.3989422804014327 * jnp.exp(-0.5 * pre * pre)
+                loaded((j, 2), (j, 3))
                 grad = (mxu(grads[j, k], weights[EXP_DEV + j]) * slope).astype(bf16)
                 pre_grad[j, k] = grad
                 entry = mxu(grad, weights[j], NT).astype(bf16)
@@ -983,7 +990,7 @@
                     summed[0, k] = entry
 
         def next_chunk(step, carry):
-            chunk(3 - step)
+            chunk(3 - step, step)
             hand(0, 3 - step)
 
             @pl.when(step > 0)
@@ -1075,7 +1082,7 @@
         unused, scaled2, invert2 = layer_norm(state_ref[...], gains_ref[1:2], biases_ref[1:2])
         loads[1].wait()
         spread_rows(cot_ref[...], padded)
-        def pick_all(which, columns, rows):
+        def pick_all(which, columns, rows, parts=(0, 1)):
             slot = lax.broadcasted_iota(jnp.int32, (PAD, capacity), 1)
 
             def picks(k, j):
@@ -1085,21 +1092,24 @@
                     hit = hit | (target_ref[rows, column : column + 1] == first)
                 return one_hot(hit)
 
-            total = mxu(picks(0, 0), returned[which, 0, 0])
-            for j in range(2):
-                for k in FAR_FIRST:
-                    if k + j > 0:
-                        total += mxu(picks(k, j), returned[which, j, k])
-            return total
+            terms = [mxu(picks(k, j), returned[which, j, k]) for j in parts for k in FAR_FIRST]
+            return sum(terms[1:], terms[0])
 
         share(0)
 
-        def one_gradient(image, carry):
+        def own_gradient(image, carry):
             rows = block_rows(image, PAD)
-            normed_part[rows, :] = pick_all(0, (0, 1), rows)
+            normed_part[rows, :] = pick_all(0, (0, 1), rows, (0,))
             return carry
 
-        lax.fori_loop(0, rows_all // PAD, one_gradient, 0)
+        def other_gradient(image, carry):
+            rows = block_rows(image, PAD)
+            normed_part[rows, :] += pick_all(0, (0, 1), rows, (1,))
+            return carry
+
+        lax.fori_loop(0, rows_all // PAD, own_gradient, 0)
+        arrive(shares[0])
+        lax.fori_loop(0, rows_all // PAD, other_gradient, 0)
         normed2_grad = normed_part[...]
         norm_own[0, 4:8] = jnp.zeros((4, D), f32)
         norm_own[0, 1:2] = jnp.sum(normed2_grad * scaled2, axis=0, keepdims=True)
@@ -1111,7 +1121,10 @@
             copy.wait()
 
         local_ref[:, qcols:] = mxu(state_low, gift_ref[...], TN)
+        for k in range(4):
+            outer[k] = local_ref[block_rows(peer(dp_here, k), shard_rows), qcols:].astype(bf16)
         out_grad_ref[...] = mxu(state_low, weight_ref[:, qcols:]).astype(bf16)
+        outward_sums = to_dp(5, lambda k: outer.at[k], lambda k: outer_in.at[k - 1])
         heads_here = qcols // (3 * HD)
         scale = HD ** (-0.5)
 
@@ -1142,9 +1155,9 @@
         normed1, scaled1, invert1 = layer_norm(normed_part[...], gains_ref[0:1], biases_ref[0:1])
         local_ref[:, :qcols] = mxu(normed1.astype(bf16), qkv_grad_ref[...], TN)
         for k in range(4):
-            inner[k] = local_ref[block_rows(peer(dp_here, k), shard_rows), :].astype(bf16)
+            inner[k] = local_ref[block_rows(peer(dp_here, k), shard_rows), :qcols].astype(bf16)
         normed_part[...] = mxu(qkv_grad_ref[...], weight_ref[:, :qcols], NT)
-        rows_sums = to_dp(1, lambda k: inner.at[k], lambda k: inner_in.at[k - 1])
+        rows_sums = to_dp(1, lambda k: inner.at[k], lambda k: inner_in.at[k - 1]) + outward_sums
         pair = Copy(
             lambda: (normed_part, normed_other, pair_send.at[0], pair_recv.at[0], partner)
         )
@@ -1152,6 +1165,7 @@
         far = pass_on(near)
 
         share(1)
+        arrive(shares[1])
 
         def one_output(image, carry):
             rows = block_rows(image, PAD)
@@ -1194,12 +1208,17 @@
     rows_sums, norms, far = travelling
 
     arrive(rows_sums)
-    plane[...] = (
-        inner[0].astype(f32)
-        + inner_in[0].astype(f32)
-        + inner_in[1].astype(f32)
-        + inner_in[2].astype(f32)
-    ).astype(bf16)
+    qcols = inner.shape[2]
+    for columns, own, got in (
+        (slice(0, qcols), inner, inner_in),
+        (slice(qcols, None), outer, outer_in),
+    ):
+        plane[:, columns] = (
+            own[0].astype(f32)
+            + got[0].astype(f32)
+            + got[1].astype(f32)
+            + got[2].astype(f32)
+        ).astype(bf16)
     quarter_rows = quarter.shape[0]
     my_quarter = block_rows(expert_here, quarter_rows)
     quarters = to_expert(
@@ -1253,7 +1272,6 @@
             arrive(totals)
             total = plane_total[...].astype(f32)
             attend_grad_ref[...] = total
-            qcols = inward_moment_ref.shape[1]
             whole_own[:, :qcols] = (0.95 * inward_moment_ref[...] + total[:, :qcols]).astype(bf16)
             whole_own[:, qcols:] = (0.95 * outward_moment_ref[...] + total[:, qcols:]).astype(bf16)
             attend_whole_ref[here, :] = whole_own[...]
@@ -1642,8 +1660,10 @@
             pltpu.VMEM((D, width), bf16),
             rows_f32,
             rows_f32,
-            pltpu.VMEM((4, shard_rows, width), bf16),
-            pltpu.VMEM((3, shard_rows, width), bf16),
+            pltpu.VMEM((4, shard_rows, qcols), bf16),
+            pltpu.VMEM((3, shard_rows, qcols), bf16),
+            pltpu.VMEM((4, shard_rows, width - qcols), bf16),
+            pltpu.VMEM((3, shard_rows, width - qcols), bf16),
             rows_low,
             pltpu.VMEM((3, shard_rows // 4, width), bf16),
             pltpu.VMEM((shard_rows // 4, width), bf16),
@@ -1656,7 +1676,7 @@
         ]
         + [dma((2, 4))] * 6
         + [dma((2,))] * 2
-        + [dma((5, 3))] * 2
+        + [dma((6, 3))] * 2
         + [dma((3, 3))] * 2
         + [dma((2, 2))] * 2
         + [dma((2,))] * 2

time: 209 us -> 208 us (level)
  no operation moved by 1% of the time
where the time goes in v2:
time: 208 us; the launch traced here: 207 us
  Pallas kernels  206 us (99%)
    pallas_call x1, Pallas kernels, pair_body(): pl.pallas_call(back_kernel, out_shape=(shape((token_rows, D), f32), shape...  112 us
    pallas_call x1, Pallas kernels, pair_body(): pl.pallas_call(front_kernel, out_shape=(shape((padded_rows, D), f32), sha...  62.9 us
    pallas_call x1, Pallas kernels, pair_body(): pl.pallas_call(finish_kernel, out_shape=(shape((4, shard_rows, width), bf...  21.1 us
    pallas_call x1, Pallas kernels, pair_body(): pl.pallas_call(apply_kernel, grid=(blocks,), out_shape=tuple([shape((toke...  9.79 us

profile of v2, /device:TPU:0, one launch (start us, length us, event | category | flops | bytes accessed | tf_op | source)
XLA Modules:
  0.0 207.4 jit_solution(9109688840709014144)
XLA Ops:
  0.7 62.9 %front.1 = (f32[832,512]{1,0:T(8,128)}, bf16[1344,256]{1,0:T(8,128)(2,1)}, bf16[832,768]{1,0:T(8,128)(2,1)}, f32[16,208,208]{2,1,0:T(8,128)}, bf16[512,1024]{1,0...) custom-call(s32[2,788]{1,0:T(2,128)} %bitcast.78, ...), custom_call_target="tpu_custom_call" | custom-call | flops 60000002048 | bytes 30000000 | tf_op jit(solution)/shard_map/front/pallas_call | solution.py:1570
  63.6 112.1 %back.1 = (f32[788,512]{1,0:T(8,128)}, bf16[788,512]{1,0:T(8,128)(2,1)}, f32[4,512]{1,0:T(4,128)}, f32[128,1024]{1,0:T(8,128)}, bf16[512,1024]{1,0:T(8,128)(2,1)...) custom-call(f32[832,2]{1,0:T(8,128)} %get-tuple-element.68.combine_ref, ...), custom_call_target="tpu_custom_call" | custom-call | flops 109999996928 | bytes 60000000 | tf_op jit(solution)/shard_map/back/pallas_call | solution.py:1637
  175.7 21.1 %finish.1 = (bf16[4,128,1024]{2,1,0:T(8,128)(2,1)}, f32[128,1024]{1,0:T(8,128)}) custom-call(bf16[512,1024]{1,0:T(8,128)(2,1)} %get-tuple-element.79.whole_ref, bf16[512,1024]{1,0:T(8,128)(2,1)} %get-tuple-element.80.own_steps_ref), custom_call_target="tpu_custom_call" | custom-call | flops 20000000000 | bytes 5000000 | tf_op jit(solution)/shard_map/finish/pallas_call | solution.py:1712
  197.4 9.8 %apply.1 = (bf16[788,512]{1,0:T(8,128)(2,1)}, f32[788,512]{1,0:T(8,128)}, f32[128,768]{1,0:T(8,128)}, f32[128,256]{1,0:T(8,128)}, f32[2048,128]{1,0:T(8,128)}, /...) custom-call(s32[1]{0:T(128)S(6)} %copy.53.steps_done_ref, ...), custom_call_target="tpu_custom_call" | custom-call | flops 20000000 | bytes 20000000 | tf_op jit(solution)/shard_map/apply/pallas_call | solution.py:1742

commit v3 on v2

--- a/solution.py
+++ b/solution.py
@@ -344,9 +344,10 @@
 
 
 def spread_rows(value, padded_ref):
-    padded_ref[...] = jnp.zeros_like(padded_ref)
+    tail = jnp.zeros((PAD - SEQ, value.shape[1]), value.dtype)
     for image in range(value.shape[0] // SEQ):
         padded_ref[image * PAD : image * PAD + SEQ, :] = value[image * SEQ : (image + 1) * SEQ]
+        padded_ref[image * PAD + SEQ : (image + 1) * PAD, :] = tail
 
 
 def gather_rows(padded, out_ref):

time: 208 us -> 207 us (level)
  no operation moved by 1% of the time
where the time goes in v3:
time: 207 us
  Pallas kernels  206 us (100%)
    pallas_call x1, Pallas kernels, pair_body(): pl.pallas_call(back_kernel, out_shape=(shape((token_rows, D), f32), shape...  112 us
    pallas_call x1, Pallas kernels, pair_body(): pl.pallas_call(front_kernel, out_shape=(shape((padded_rows, D), f32), sha...  62.9 us
    pallas_call x1, Pallas kernels, pair_body(): pl.pallas_call(finish_kernel, out_shape=(shape((4, shard_rows, width), bf...  21.1 us
    pallas_call x1, Pallas kernels, pair_body(): pl.pallas_call(apply_kernel, grid=(blocks,), out_shape=tuple([shape((toke...  9.79 us

profile of v3, /device:TPU:0, one launch (start us, length us, event | category | flops | bytes accessed | tf_op | source)
XLA Modules:
  0.0 207.2 jit_solution(4015868732370264228)
XLA Ops:
  0.7 62.9 %front.1 = (f32[832,512]{1,0:T(8,128)}, bf16[1344,256]{1,0:T(8,128)(2,1)}, bf16[832,768]{1,0:T(8,128)(2,1)}, f32[16,208,208]{2,1,0:T(8,128)}, bf16[512,1024]{1,0...) custom-call(s32[2,788]{1,0:T(2,128)} %bitcast.78, ...), custom_call_target="tpu_custom_call" | custom-call | flops 60000002048 | bytes 30000000 | tf_op jit(solution)/shard_map/front/pallas_call | solution.py:1571
  63.5 111.9 %back.1 = (f32[788,512]{1,0:T(8,128)}, bf16[788,512]{1,0:T(8,128)(2,1)}, f32[4,512]{1,0:T(4,128)}, f32[128,1024]{1,0:T(8,128)}, bf16[512,1024]{1,0:T(8,128)(2,1)...) custom-call(f32[832,2]{1,0:T(8,128)} %get-tuple-element.68.combine_ref, ...), custom_call_target="tpu_custom_call" | custom-call | flops 109999996928 | bytes 60000000 | tf_op jit(solution)/shard_map/back/pallas_call | solution.py:1638
  175.5 21.1 %finish.1 = (bf16[4,128,1024]{2,1,0:T(8,128)(2,1)}, f32[128,1024]{1,0:T(8,128)}) custom-call(bf16[512,1024]{1,0:T(8,128)(2,1)} %get-tuple-element.79.whole_ref, bf16[512,1024]{1,0:T(8,128)(2,1)} %get-tuple-element.80.own_steps_ref), custom_call_target="tpu_custom_call" | custom-call | flops 20000000000 | bytes 5000000 | tf_op jit(solution)/shard_map/finish/pallas_call | solution.py:1713
  197.2 9.8 %apply.1 = (bf16[788,512]{1,0:T(8,128)(2,1)}, f32[788,512]{1,0:T(8,128)}, f32[128,768]{1,0:T(8,128)}, f32[128,256]{1,0:T(8,128)}, f32[2048,128]{1,0:T(8,128)}, /...) custom-call(s32[1]{0:T(128)S(6)} %copy.53.steps_done_ref, ...), custom_call_target="tpu_custom_call" | custom-call | flops 20000000 | bytes 20000000 | tf_op jit(solution)/shard_map/apply/pallas_call | solution.py:1743
